TPU v7x, 32 devices: a whole 2x2x4 slice. The times are simulated.
32 devices in a mesh: sub: 8 (over z, y), slab: 4 (over x, core).
Axes of the slice: x: 2, y: 2, z: 4, core: 2. Of those that a mesh axis runs over, the one named last changes fastest.
Arguments:
- rhs: float32 [8, 64, 8, 512], P(None, 'sub', None, 'slab'), may hold values from -60 to 60, as said below
- perm: float32 [64, 8, 512], P('sub', None, 'slab'), may hold values from 0.1 to 10
- accum: float32 [64, 8, 512], P('sub', None, 'slab'), may hold values from 0.05 to 0.5
- counts: int32 [8], replicated, may hold values from 1 to 8, as said below
Outputs:
- solution: float32 [8, 64, 8, 512], P(None, 'sub', None, 'slab')
- residual: float32 [8, 64, 8, 512], P(None, 'sub', None, 'slab')
Inputs may be any that keep to these rules, and one draw needn't show every extreme that they name: `rhs`: pressure sources of the 8 systems; values on planes that are not live are never read. counts[i] live planes fill the first slots of subdomain i; some subdomain has 8.
All inputs are finite; a program needn't handle non-finite values.
Results may differ from a plain program's by a relative error of at most 0.00045.
Values sent between devices are 32-bit elements; how exact they have to be, the bound alone decides.
A program may use at most 64 MiB of HBM per device.

v0:
```python
import jax
import jax.numpy as jnp
from jax import lax
from jax.sharding import PartitionSpec as P

S = 8
ITERS = 4
DEG = 4
cheb_low = 0.05
cheb_high = 2.0


def with_halo(cells, sides, width):
    for axis, dim in sides:
        count = lax.axis_size(axis)
        ends = count - 1
        head = lax.slice_in_dim(cells, 0, width, axis=dim)
        tail = lax.slice_in_dim(cells, cells.shape[dim] - width, cells.shape[dim], axis=dim)
        cells = jnp.concatenate(
            [
                lax.ppermute(tail, axis, [(i, (i + 1) % count) for i in range(ends)]),
                cells,
                lax.ppermute(head, axis, [((i + 1) % count, i) for i in range(ends)]),
            ],
            axis=dim,
        )
    return cells


def neighbours(field, live, plane):
    first = field[:, 0]
    last = lax.dynamic_index_in_dim(field, live - 1, 1, keepdims=False)
    edges = with_halo(jnp.stack([first, last], axis=1), (("sub", 1),), 1)
    before = edges[:, 0:1]
    after = edges[:, 3:4]
    zero_plane = jnp.zeros_like(field[:, :1])
    up_inside = jnp.concatenate([field[:, 1:], zero_plane], axis=1)
    down_inside = jnp.concatenate([zero_plane, field[:, :-1]], axis=1)
    x_next = jnp.where(plane == live - 1, after, up_inside)
    x_prev = jnp.where(plane == 0, before, down_inside)
    zero_row = jnp.zeros_like(field[:, :, :1])
    y_next = jnp.concatenate([field[:, :, 1:], zero_row], axis=2)
    y_prev = jnp.concatenate([zero_row, field[:, :, :-1]], axis=2)
    padded = with_halo(field, (("slab", 3),), 1)
    z_next = padded[..., 2:]
    z_prev = padded[..., :-2]
    return (x_next, x_prev, y_next, y_prev, z_next, z_prev)


def product(left, right):
    return lax.dot_general(
        left.reshape(left.shape[0], -1),
        right.reshape(right.shape[0], -1),
        (((1,), (1,)), ((), ())),
        precision=lax.Precision.HIGHEST,
    )


def combine(coef, block):
    flat = jnp.dot(coef, block.reshape(block.shape[0], -1), precision=lax.Precision.HIGHEST)
    return flat.reshape(block.shape)


def lower_solve(factor, block):
    flat = jax.scipy.linalg.solve_triangular(factor, block.reshape(block.shape[0], -1), lower=True)
    return flat.reshape(block.shape)


def precondition(vector, operate, inv_diag):
    theta = 0.5 * (cheb_high + cheb_low)
    delta = 0.5 * (cheb_high - cheb_low)
    sigma = theta / delta
    remain = vector
    update = inv_diag * remain * (1.0 / theta)
    result = update
    rho = 1.0 / sigma
    for step in range(DEG - 1):
        remain = remain - operate(update)
        rho_next = 1.0 / (2.0 * sigma - rho)
        update = rho_next * rho * update + 2.0 * rho_next / delta * (inv_diag * remain)
        result = result + update
        rho = rho_next
    return result


def small_solve(coefs, lowers, lead):
    hess = jnp.zeros((ITERS * S, (ITERS + 1) * S), jnp.float32)
    for j in range(ITERS):
        for i in range(j + 1):
            hess = hess.at[j * S : (j + 1) * S, i * S : (i + 1) * S].set(coefs[j][i])
        hess = hess.at[j * S : (j + 1) * S, (j + 1) * S : (j + 2) * S].set(lowers[j])
    target = jnp.zeros((S, (ITERS + 1) * S), jnp.float32).at[:, :S].set(lead)
    normal = jnp.dot(hess, hess.T, precision=lax.Precision.HIGHEST)
    right = jnp.dot(hess, target.T, precision=lax.Precision.HIGHEST)
    factor = jnp.linalg.cholesky(normal)
    mix = jax.scipy.linalg.cho_solve((factor, True), right).T
    return (mix, hess, target)


def body(rhs, perm, accum, counts):
    live = counts[lax.axis_index("sub")]
    depth = rhs.shape[1]
    plane = lax.broadcasted_iota(jnp.int32, (1, depth, 1, 1), 1)
    mask = (plane < live).astype(jnp.float32)
    field_perm = perm[None]
    near = neighbours(field_perm, live, plane)
    conduct = []
    diag = accum[None]
    for other in near:
        weight = 2.0 * field_perm * other / (field_perm + other)
        conduct.append(weight)
        diag = diag + weight
    inv_diag = mask / diag

    def operate(field):
        beside = neighbours(field, live, plane)
        total = diag * field
        for weight, other in zip(conduct, beside):
            total = total - weight * other
        return mask * total

    start = rhs * mask
    lead = jnp.linalg.cholesky(lax.psum(product(start, start), ("sub", "slab")))
    basis = [lower_solve(lead, start)]
    coefs = []
    lowers = []
    for step in range(ITERS):
        direction = precondition(basis[step], operate, inv_diag)
        work = operate(direction)
        stacked, whole = lax.psum(
            (jnp.stack([product(work, basis[i]) for i in range(step + 1)]), product(work, work)),
            ("sub", "slab"),
        )
        found = [stacked[i] for i in range(step + 1)]
        block = whole
        for i in range(step + 1):
            work = work - combine(found[i], basis[i])
            block = block - jnp.dot(found[i], found[i].T, precision=lax.Precision.HIGHEST)
        lower = jnp.linalg.cholesky(block)
        basis.append(lower_solve(lower, work))
        coefs.append(found)
        lowers.append(lower)
    mix, hess, target = small_solve(coefs, lowers, lead)
    combo = combine(mix[:, :S], basis[0])
    for j in range(1, ITERS):
        combo = combo + combine(mix[:, j * S : (j + 1) * S], basis[j])
    solution = precondition(combo, operate, inv_diag)
    residual = start - operate(solution)
    return (solution, residual)


def solution(mesh):
    placed = (P(None, "sub", None, "slab"), P("sub", None, "slab"), P("sub", None, "slab"), P())
    return jax.shard_map(
        body,
        mesh=mesh,
        in_specs=placed,
        out_specs=(P(None, "sub", None, "slab"), P(None, "sub", None, "slab")),
        check_vma=False,
    )
```

profile of v0, /device:TPU:2, one launch (start us, length us, event | category | flops | bytes accessed | tf_op | source)
XLA Modules:
  0.0 579.4 jit_solution(9655729661371559790)
XLA Ops:
  16.0 42.4 %psum.63 = f32[8,8]{0,1:T(8,128)S(1)} all-reduce(f32[8,8]{0,1:T(8,128)S(1)} %convolution_bitcast_fusion.13), channel_id=1, replica_groups=mesh['sub'=8,'slab'=4] {'sub','slab'}, use_global_device_ids=true, to_apply=%region_0.1 | all-reduce | flops 64 | bytes 512 | tf_op jit(solution)/shard_map/psum | solution.py:123
  74.7 4.2 collective-permute-done.4
  85.2 4.4 collective-permute-start.9
  91.2 4.2 collective-permute-done.8
  106.6 4.2 collective-permute-done.12
  122.8 4.2 collective-permute-done.16
  128.8 39.8 %all-reduce.89 = (f32[8,8]{1,0:T(8,128)S(1)}, f32[8,8]{0,1:T(8,128)S(1)}) all-reduce(f32[8,8]{1,0:T(8,128)S(1)} %fusion.290, f32[8,8]{0,1:T(8,128)S(1)} %convolution_bitcast_fusion.12), channel_id=1, replica_groups=mesh['sub'=8,'slab'=4] {'sub','slab'}, use_global_device_ids=true, to_apply=%region_3.6 | all-reduce | flops 128 | bytes 1024 | tf_op jit(solution)/shard_map/psum | solution.py:130
  195.8 4.8 collective-permute-start.25
  202.2 4.2 collective-permute-done.24
  217.1 4.2 collective-permute-done.28
  233.1 4.2 collective-permute-done.32
  239.8 39.4 %all-reduce.88 = (f32[2,8,8]{2,1,0:T(8,128)S(1)}, f32[8,8]{0,1:T(8,128)S(1)}) all-reduce(f32[2,8,8]{2,1,0:T(8,128)S(1)} %pad_maximum_fusion.44, f32[8,8]{0,1:T(8,128)S(1)} %convolution_bitcast_fusion.9), channel_id=1, replica_groups=mesh['sub'=8,'slab'=4] {'sub','slab'}, use_global_device_ids=true, to_apply=%region_6.9 | all-reduce | flops 192 | bytes 1536 | tf_op jit(solution)/shard_map/psum | solution.py:130
  305.0 4.8 collective-permute-start.41
  311.4 4.2 collective-permute-done.40
  326.4 4.2 collective-permute-done.44
  342.3 4.2 collective-permute-done.48
  349.8 39.5 %all-reduce.87 = (f32[3,8,8]{2,1,0:T(8,128)S(1)}, f32[8,8]{0,1:T(8,128)S(1)}) all-reduce(f32[3,8,8]{2,1,0:T(8,128)S(1)} %pad_maximum_fusion.43, f32[8,8]{0,1:T(8,128)S(1)} %convolution_bitcast_fusion.5), channel_id=1, replica_groups=mesh['sub'=8,'slab'=4] {'sub','slab'}, use_global_device_ids=true, to_apply=%region_8.11 | all-reduce | flops 256 | bytes 2048 | tf_op jit(solution)/shard_map/psum | solution.py:130
  415.6 4.8 collective-permute-start.57
  422.0 4.2 collective-permute-done.56
  452.9 4.2 collective-permute-done.64
  461.1 39.9 %all-reduce.86 = (f32[4,8,8]{2,1,0:T(8,128)S(1)}, f32[8,8]{0,1:T(8,128)S(1)}) all-reduce(f32[4,8,8]{2,1,0:T(8,128)S(1)} %pad_maximum_fusion.42, f32[8,8]{0,1:T(8,128)S(1)} %convolution_bitcast_fusion), channel_id=1, replica_groups=mesh['sub'=8,'slab'=4] {'sub','slab'}, use_global_device_ids=true, to_apply=%region_10.13 | all-reduce | flops 320 | bytes 2560 | tf_op jit(solution)/shard_map/psum | solution.py:130
  525.3 4.7 collective-permute-done.68
  536.3 4.8 collective-permute-start.73
  557.5 4.2 collective-permute-done.76
  (387 shorter events, 290.5 us)
Async XLA Ops:
  1.6 61.9 %collective-permute-start.3 = (f32[1,8,8,1]{3,2,1,0:T(8,128)S(1)}, f32[1,8,8,1]{3,2,1,0:T(8,128)S(1)}, u32[]{:S(2)}, u32[]{:S(2)}) collective-permute-start(f32[1,8,8,1]{3,2,1,0:T(8,128)S(1)} %get-tuple-element.393), channel_id=1, source_target_pairs={{0,1},{1,2},{2,3},{4,5},{5,6},{6,7},{8,9},{9,10},{10,11},{12,13},{... | collective-permute-start | bytes 776 | tf_op jit(solution)/shard_map/ppermute | solution.py:21
  3.5 60.0 %collective-permute-start.2 = (f32[1,8,8,1]{3,2,1,0:T(8,128)S(1)}, f32[1,8,8,1]{3,2,1,0:T(8,128)S(1)}, u32[]{:S(2)}, u32[]{:S(2)}) collective-permute-start(f32[1,8,8,1]{3,2,1,0:T(8,128)S(1)} %get-tuple-element.392), channel_id=1, source_target_pairs={{1,0},{2,1},{3,2},{5,4},{6,5},{7,6},{9,8},{10,9},{11,10},{13,12},{... | collective-permute-start | bytes 776 | tf_op jit(solution)/shard_map/ppermute | solution.py:23
  9.1 54.4 %collective-permute-start.1 = (f32[1,1,8,128]{3,2,1,0:T(8,128)S(1)}, f32[1,1,8,128]{3,2,1,0:T(8,128)S(1)}, u32[]{:S(2)}, u32[]{:S(2)}) collective-permute-start(f32[1,1,8,128]{3,2,1,0:T(8,128)S(1)} %fusion.154), channel_id=1, source_target_pairs={{0,4},{4,8},{8,12},{12,16},{16,20},{20,24},{24,28},{1,5},{5,9},{9,... | collective-permute-start | bytes 12296 | tf_op jit(solution)/shard_map/ppermute | solution.py:21
  12.6 51.0 %collective-permute-start = (f32[1,1,8,128]{3,2,1,0:T(8,128)S(1)}, f32[1,1,8,128]{3,2,1,0:T(8,128)S(1)}, u32[]{:S(2)}, u32[]{:S(2)}) collective-permute-start(f32[1,1,8,128]{3,2,1,0:T(8,128)S(1)} %slice.1210), channel_id=1, source_target_pairs={{4,0},{8,4},{12,8},{16,12},{20,16},{24,20},{28,24},{5,1},{9,5},{13... | collective-permute-start | bytes 12296 | tf_op jit(solution)/shard_map/ppermute | solution.py:23
  64.3 10.3 %collective-permute-start.7 = (f32[8,8,8,1]{3,0,2,1:T(8,128)S(1)}, f32[8,8,8,1]{3,0,2,1:T(8,128)S(1)}, u32[]{:S(2)}, u32[]{:S(2)}) collective-permute-start(f32[8,8,8,1]{3,0,2,1:T(8,128)S(1)} %get-tuple-element.379), channel_id=1, source_target_pairs={{0,1},{1,2},{2,3},{4,5},{5,6},{6,7},{8,9},{9,10},{10,11},{12,13},{... | collective-permute-start | bytes 6152 | tf_op jit(solution)/shard_map/ppermute | solution.py:21
  79.6 11.4 %collective-permute-start.11 = (f32[8,8,8,1]{3,0,2,1:T(8,128)S(1)}, f32[8,8,8,1]{3,0,2,1:T(8,128)S(1)}, u32[]{:S(2)}, u32[]{:S(2)}) collective-permute-start(f32[8,8,8,1]{3,0,2,1:T(8,128)S(1)} %get-tuple-element.371), channel_id=1, source_target_pairs={{0,1},{1,2},{2,3},{4,5},{5,6},{6,7},{8,9},{9,10},{10,11},{12,13},{... | collective-permute-start | bytes 6152 | tf_op jit(solution)/shard_map/ppermute | solution.py:21
  96.0 10.3 %collective-permute-start.15 = (f32[8,8,8,1]{3,0,2,1:T(8,128)S(1)}, f32[8,8,8,1]{3,0,2,1:T(8,128)S(1)}, u32[]{:S(2)}, u32[]{:S(2)}) collective-permute-start(f32[8,8,8,1]{3,0,2,1:T(8,128)S(1)} %get-tuple-element.363), channel_id=1, source_target_pairs={{0,1},{1,2},{2,3},{4,5},{5,6},{6,7},{8,9},{9,10},{10,11},{12,13},{... | collective-permute-start | bytes 6152 | tf_op jit(solution)/shard_map/ppermute | solution.py:21
  111.5 11.1 %collective-permute-start.19 = (f32[8,8,8,1]{3,0,2,1:T(8,128)S(1)}, f32[8,8,8,1]{3,0,2,1:T(8,128)S(1)}, u32[]{:S(2)}, u32[]{:S(2)}) collective-permute-start(f32[8,8,8,1]{3,0,2,1:T(8,128)S(1)} %get-tuple-element.355), channel_id=1, source_target_pairs={{0,1},{1,2},{2,3},{4,5},{5,6},{6,7},{8,9},{9,10},{10,11},{12,13},{... | collective-permute-start | bytes 6152 | tf_op jit(solution)/shard_map/ppermute | solution.py:21
  175.2 11.4 %collective-permute-start.23 = (f32[8,8,8,1]{3,0,2,1:T(8,128)}, f32[8,8,8,1]{3,0,2,1:T(8,128)S(1)}, u32[]{:S(2)}, u32[]{:S(2)}) collective-permute-start(f32[8,8,8,1]{3,0,2,1:T(8,128)} %get-tuple-element.347), channel_id=1, source_target_pairs={{0,1},{1,2},{2,3},{4,5},{5,6},{6,7},{8,9},{9,10},{10,11},{12,13},{... | collective-permute-start | bytes 6152 | tf_op jit(solution)/shard_map/ppermute | solution.py:21
  190.2 11.8 %collective-permute-start.27 = (f32[8,8,8,1]{3,0,2,1:T(8,128)S(1)}, f32[8,8,8,1]{3,0,2,1:T(8,128)S(1)}, u32[]{:S(2)}, u32[]{:S(2)}) collective-permute-start(f32[8,8,8,1]{3,0,2,1:T(8,128)S(1)} %get-tuple-element.339), channel_id=1, source_target_pairs={{0,1},{1,2},{2,3},{4,5},{5,6},{6,7},{8,9},{9,10},{10,11},{12,13},{... | collective-permute-start | bytes 6152 | tf_op jit(solution)/shard_map/ppermute | solution.py:21
  207.0 9.9 %collective-permute-start.31 = (f32[8,8,8,1]{3,0,2,1:T(8,128)S(1)}, f32[8,8,8,1]{3,0,2,1:T(8,128)S(1)}, u32[]{:S(2)}, u32[]{:S(2)}) collective-permute-start(f32[8,8,8,1]{3,0,2,1:T(8,128)S(1)} %get-tuple-element.331), channel_id=1, source_target_pairs={{0,1},{1,2},{2,3},{4,5},{5,6},{6,7},{8,9},{9,10},{10,11},{12,13},{... | collective-permute-start | bytes 6152 | tf_op jit(solution)/shard_map/ppermute | solution.py:21
  222.0 11.0 %collective-permute-start.35 = (f32[8,8,8,1]{3,0,2,1:T(8,128)S(1)}, f32[8,8,8,1]{3,0,2,1:T(8,128)S(1)}, u32[]{:S(2)}, u32[]{:S(2)}) collective-permute-start(f32[8,8,8,1]{3,0,2,1:T(8,128)S(1)} %get-tuple-element.323), channel_id=1, source_target_pairs={{0,1},{1,2},{2,3},{4,5},{5,6},{6,7},{8,9},{9,10},{10,11},{12,13},{... | collective-permute-start | bytes 6152 | tf_op jit(solution)/shard_map/ppermute | solution.py:21
  284.4 11.4 %collective-permute-start.39 = (f32[8,8,8,1]{3,0,2,1:T(8,128)}, f32[8,8,8,1]{3,0,2,1:T(8,128)S(1)}, u32[]{:S(2)}, u32[]{:S(2)}) collective-permute-start(f32[8,8,8,1]{3,0,2,1:T(8,128)} %get-tuple-element.315), channel_id=1, source_target_pairs={{0,1},{1,2},{2,3},{4,5},{5,6},{6,7},{8,9},{9,10},{10,11},{12,13},{... | collective-permute-start | bytes 6152 | tf_op jit(solution)/shard_map/ppermute | solution.py:21
  299.4 11.8 %collective-permute-start.43 = (f32[8,8,8,1]{3,0,2,1:T(8,128)S(1)}, f32[8,8,8,1]{3,0,2,1:T(8,128)S(1)}, u32[]{:S(2)}, u32[]{:S(2)}) collective-permute-start(f32[8,8,8,1]{3,0,2,1:T(8,128)S(1)} %get-tuple-element.307), channel_id=1, source_target_pairs={{0,1},{1,2},{2,3},{4,5},{5,6},{6,7},{8,9},{9,10},{10,11},{12,13},{... | collective-permute-start | bytes 6152 | tf_op jit(solution)/shard_map/ppermute | solution.py:21
  316.3 9.9 %collective-permute-start.47 = (f32[8,8,8,1]{3,0,2,1:T(8,128)S(1)}, f32[8,8,8,1]{3,0,2,1:T(8,128)S(1)}, u32[]{:S(2)}, u32[]{:S(2)}) collective-permute-start(f32[8,8,8,1]{3,0,2,1:T(8,128)S(1)} %get-tuple-element.299), channel_id=1, source_target_pairs={{0,1},{1,2},{2,3},{4,5},{5,6},{6,7},{8,9},{9,10},{10,11},{12,13},{... | collective-permute-start | bytes 6152 | tf_op jit(solution)/shard_map/ppermute | solution.py:21
  331.3 10.8 %collective-permute-start.51 = (f32[8,8,8,1]{3,0,2,1:T(8,128)S(1)}, f32[8,8,8,1]{3,0,2,1:T(8,128)S(1)}, u32[]{:S(2)}, u32[]{:S(2)}) collective-permute-start(f32[8,8,8,1]{3,0,2,1:T(8,128)S(1)} %get-tuple-element.291), channel_id=1, source_target_pairs={{0,1},{1,2},{2,3},{4,5},{5,6},{6,7},{8,9},{9,10},{10,11},{12,13},{... | collective-permute-start | bytes 6152 | tf_op jit(solution)/shard_map/ppermute | solution.py:21
  395.0 12.2 %collective-permute-start.55 = (f32[8,8,8,1]{3,0,2,1:T(8,128)}, f32[8,8,8,1]{3,0,2,1:T(8,128)S(1)}, u32[]{:S(2)}, u32[]{:S(2)}) collective-permute-start(f32[8,8,8,1]{3,0,2,1:T(8,128)} %get-tuple-element.283), channel_id=1, source_target_pairs={{0,1},{1,2},{2,3},{4,5},{5,6},{6,7},{8,9},{9,10},{10,11},{12,13},{... | collective-permute-start | bytes 6152 | tf_op jit(solution)/shard_map/ppermute | solution.py:21
  396.9 10.3 %collective-permute-start.54 = (f32[8,8,8,1]{3,0,2,1:T(8,128)}, f32[8,8,8,1]{3,0,2,1:T(8,128)S(1)}, u32[]{:S(2)}, u32[]{:S(2)}) collective-permute-start(f32[8,8,8,1]{3,0,2,1:T(8,128)} %get-tuple-element.282), channel_id=1, source_target_pairs={{1,0},{2,1},{3,2},{5,4},{6,5},{7,6},{9,8},{10,9},{11,10},{13,12},{... | collective-permute-start | bytes 6152 | tf_op jit(solution)/shard_map/ppermute | solution.py:23
  410.0 11.8 %collective-permute-start.59 = (f32[8,8,8,1]{3,0,2,1:T(8,128)S(1)}, f32[8,8,8,1]{3,0,2,1:T(8,128)S(1)}, u32[]{:S(2)}, u32[]{:S(2)}) collective-permute-start(f32[8,8,8,1]{3,0,2,1:T(8,128)S(1)} %get-tuple-element.275), channel_id=1, source_target_pairs={{0,1},{1,2},{2,3},{4,5},{5,6},{6,7},{8,9},{9,10},{10,11},{12,13},{... | collective-permute-start | bytes 6152 | tf_op jit(solution)/shard_map/ppermute | solution.py:21
  411.9 9.8 %collective-permute-start.58 = (f32[8,8,8,1]{3,0,2,1:T(8,128)S(1)}, f32[8,8,8,1]{3,0,2,1:T(8,128)S(1)}, u32[]{:S(2)}, u32[]{:S(2)}) collective-permute-start(f32[8,8,8,1]{3,0,2,1:T(8,128)S(1)} %get-tuple-element.274), channel_id=1, source_target_pairs={{1,0},{2,1},{3,2},{5,4},{6,5},{7,6},{9,8},{10,9},{11,10},{13,12},{... | collective-permute-start | bytes 6152 | tf_op jit(solution)/shard_map/ppermute | solution.py:23
  426.8 10.3 %collective-permute-start.63 = (f32[8,8,8,1]{3,0,2,1:T(8,128)S(1)}, f32[8,8,8,1]{3,0,2,1:T(8,128)S(1)}, u32[]{:S(2)}, u32[]{:S(2)}) collective-permute-start(f32[8,8,8,1]{3,0,2,1:T(8,128)S(1)} %get-tuple-element.267), channel_id=1, source_target_pairs={{0,1},{1,2},{2,3},{4,5},{5,6},{6,7},{8,9},{9,10},{10,11},{12,13},{... | collective-permute-start | bytes 6152 | tf_op jit(solution)/shard_map/ppermute | solution.py:21
  442.2 10.4 %collective-permute-start.67 = (f32[8,8,8,1]{3,0,2,1:T(8,128)S(1)}, f32[8,8,8,1]{3,0,2,1:T(8,128)S(1)}, u32[]{:S(2)}, u32[]{:S(2)}) collective-permute-start(f32[8,8,8,1]{3,0,2,1:T(8,128)S(1)} %get-tuple-element.259), channel_id=1, source_target_pairs={{0,1},{1,2},{2,3},{4,5},{5,6},{6,7},{8,9},{9,10},{10,11},{12,13},{... | collective-permute-start | bytes 6152 | tf_op jit(solution)/shard_map/ppermute | solution.py:21
  530.7 11.8 %collective-permute-start.75 = (f32[8,8,8,1]{3,0,2,1:T(8,128)S(1)}, f32[8,8,8,1]{3,0,2,1:T(8,128)S(1)}, u32[]{:S(2)}, u32[]{:S(2)}) collective-permute-start(f32[8,8,8,1]{3,0,2,1:T(8,128)S(1)} %get-tuple-element.243), channel_id=1, source_target_pairs={{0,1},{1,2},{2,3},{4,5},{5,6},{6,7},{8,9},{9,10},{10,11},{12,13},{... | collective-permute-start | bytes 6152 | tf_op jit(solution)/shard_map/ppermute | solution.py:21
  562.4 11.7 %collective-permute-start.83 = (f32[8,8,8,1]{3,0,2,1:T(8,128)S(1)}, f32[8,8,8,1]{3,0,2,1:T(8,128)S(1)}, u32[]{:S(2)}, u32[]{:S(2)}) collective-permute-start(f32[8,8,8,1]{3,0,2,1:T(8,128)S(1)} %get-tuple-element.227), channel_id=1, source_target_pairs={{0,1},{1,2},{2,3},{4,5},{5,6},{6,7},{8,9},{9,10},{10,11},{12,13},{... | collective-permute-start | bytes 6152 | tf_op jit(solution)/shard_map/ppermute | solution.py:21
  (65 other events, 437.3 us)
where the time goes:
time: 591 us; the launch traced here: 579 us
  starting transfers between devices  221 us (37%)
  blocking collectives  201 us (34%)
  waiting for transfers between devices  83.3 us (14%)
  other arithmetic  33.3 us (6%)
  local copies, waits for them, and re-layouts  18.9 us (3%)
  matrix products  17.9 us (3%)
    psum x4, blocking collectives, body(): lax.psum((jnp.stack([product(work, basis[i]) for i in range(step + 1)]),...  159 us
    ppermute x42, starting transfers between devices, with_halo(): lax.ppermute(tail, axis, [(i, (i + 1) % count) for i in range(ends)])  117 us
    ppermute x42, starting transfers between devices, with_halo(): lax.ppermute(head, axis, [((i + 1) % count, i) for i in range(ends)])  104 us
    ppermute x42, waiting for transfers between devices, with_halo(): lax.ppermute(head, axis, [((i + 1) % count, i) for i in range(ends)])  80.1 us
    psum x1, blocking collectives, body(): lead = jnp.linalg.cholesky(lax.psum(product(start, start), ('sub', 'slab')))  42.4 us
  transfers between devices with their start and end apart: 84, of which 35 were waited for; matrix products, arithmetic and copies ran while one was open for 3% of the time, Pallas kernels for 0%

commit v1 on v0

--- a/solution.py
+++ b/solution.py
@@ -128,8 +128,14 @@
         direction = precondition(basis[step], operate, inv_diag)
         work = operate(direction)
         stacked, whole = lax.psum(
-            (jnp.stack([product(work, basis[i]) for i in range(step + 1)]), product(work, work)),
-            ("sub", "slab"),
+            lax.psum(
+                (
+                    jnp.stack([product(work, basis[i]) for i in range(step + 1)]),
+                    product(work, work),
+                ),
+                axis_name="slab",
+            ),
+            "sub",
         )
         found = [stacked[i] for i in range(step + 1)]
         block = whole

time: 591 us -> 573 us (0.970)
  starting transfers between devices: 221 us -> 206 us
    psum x4, blocking collectives: 159 us -> 36.4 us  [body(): lax.psum((jnp.stack([product(work, basis[i]) for i in range(step + 1)]),...]
    psum x0 -> x4, blocking collectives: none -> 120 us  [body(): lax.psum(lax.psum((jnp.stack([product(work, basis[i]) for i in range(step...]
    ppermute x42, starting transfers between devices: 117 us -> 102 us  [with_halo(): lax.ppermute(tail, axis, [(i, (i + 1) % count) for i in range(ends)])]
where the time goes in v1:
time: 573 us; the launch traced here: 562 us
  starting transfers between devices  206 us (36%)
  blocking collectives  199 us (35%)
  waiting for transfers between devices  82.3 us (14%)
  other arithmetic  33.3 us (6%)
  local copies, waits for them, and re-layouts  18.8 us (3%)
  matrix products  17.9 us (3%)
    psum x4, blocking collectives, body(): lax.psum(lax.psum((jnp.stack([product(work, basis[i]) for i in range(step...  120 us
    ppermute x42, starting transfers between devices, with_halo(): lax.ppermute(head, axis, [((i + 1) % count, i) for i in range(ends)])  104 us
    ppermute x42, starting transfers between devices, with_halo(): lax.ppermute(tail, axis, [(i, (i + 1) % count) for i in range(ends)])  102 us
    ppermute x42, waiting for transfers between devices, with_halo(): lax.ppermute(head, axis, [((i + 1) % count, i) for i in range(ends)])  79.3 us
    psum x1, blocking collectives, body(): lead = jnp.linalg.cholesky(lax.psum(product(start, start), ('sub', 'slab')))  42.4 us
    psum x4, blocking collectives, body(): lax.psum((jnp.stack([product(work, basis[i]) for i in range(step + 1)]),...  36.4 us
  transfers between devices with their start and end apart: 84, of which 35 were waited for; matrix products, arithmetic and copies ran while one was open for 3% of the time, Pallas kernels for 0%

profile of v1, /device:TPU:2, one launch (start us, length us, event | category | flops | bytes accessed | tf_op | source)
XLA Modules:
  0.0 562.2 jit_solution(10255116856603378751)
XLA Ops:
  16.0 42.4 %psum.119 = f32[8,8]{0,1:T(8,128)S(1)} all-reduce(f32[8,8]{0,1:T(8,128)S(1)} %convolution_bitcast_fusion.14), channel_id=1, replica_groups=mesh['sub'=8,'slab'=4] {'sub','slab'}, use_global_device_ids=true, to_apply=%region_0.1 | all-reduce | flops 64 | bytes 512 | tf_op jit(solution)/shard_map/psum | solution.py:123
  74.8 4.2 collective-permute-done.4
  85.2 4.4 collective-permute-start.9
  91.2 4.2 collective-permute-done.8
  106.6 4.2 collective-permute-done.12
  122.9 4.2 collective-permute-done.16
  128.8 5.9 %all-reduce.93 = (f32[1,8,8]{2,1,0:T(8,128)S(1)}, f32[8,8]{0,1:T(8,128)S(1)}) all-reduce(f32[1,8,8]{2,1,0:T(8,128)S(1)} %convolution_bitcast_fusion.13, f32[8,8]{0,1:T(8,128)S(1)} %convolution_bitcast_fusion.12), channel_id=1, replica_groups=mesh['sub'=8,'slab'=4] {'slab'}, use_global_device_ids=true, to_apply=%region_3.6 | all-reduce | flops 128 | bytes 1024 | tf_op jit(solution)/shard_map/psum | solution.py:131
  134.7 18.9 %all-reduce.89 = (f32[8,8]{1,0:T(8,128)S(1)}, f32[8,8]{0,1:T(8,128)S(1)}) all-reduce(f32[8,8]{1,0:T(8,128)S(1)} %bitcast.463, f32[8,8]{0,1:T(8,128)S(1)} %get-tuple-element.201), channel_id=1, replica_groups=mesh['sub'=8,'slab'=4] {'sub'}, use_global_device_ids=true, to_apply=%region_4.7 | all-reduce | flops 128 | bytes 1024 | tf_op jit(solution)/shard_map/psum | solution.py:130
  184.6 4.2 collective-permute-done.24
  199.5 4.2 collective-permute-done.28
  214.4 4.2 collective-permute-done.32
  221.1 10.1 %all-reduce.92 = (f32[2,8,8]{2,1,0:T(8,128)S(1)}, f32[8,8]{0,1:T(8,128)S(1)}) all-reduce(f32[2,8,8]{2,1,0:T(8,128)S(1)} %pad_maximum_fusion.44, f32[8,8]{0,1:T(8,128)S(1)} %convolution_bitcast_fusion.9), channel_id=1, replica_groups=mesh['sub'=8,'slab'=4] {'slab'}, use_global_device_ids=true, to_apply=%region_8.11 | all-reduce | flops 192 | bytes 1536 | tf_op jit(solution)/shard_map/psum | solution.py:131
  231.2 33.8 %all-reduce.88 = (f32[2,8,8]{2,1,0:T(8,128)S(1)}, f32[8,8]{0,1:T(8,128)S(1)}) all-reduce(f32[2,8,8]{2,1,0:T(8,128)S(1)} %get-tuple-element.198, f32[8,8]{0,1:T(8,128)S(1)} %get-tuple-element.199), channel_id=1, replica_groups=mesh['sub'=8,'slab'=4] {'sub'}, use_global_device_ids=true, to_apply=%region_9.12 | all-reduce | flops 192 | bytes 1536 | tf_op jit(solution)/shard_map/psum | solution.py:130
  294.3 4.2 collective-permute-done.40
  309.1 4.2 collective-permute-done.44
  324.0 4.2 collective-permute-done.48
  331.5 10.1 %all-reduce.91 = (f32[3,8,8]{2,1,0:T(8,128)S(1)}, f32[8,8]{0,1:T(8,128)S(1)}) all-reduce(f32[3,8,8]{2,1,0:T(8,128)S(1)} %pad_maximum_fusion.43, f32[8,8]{0,1:T(8,128)S(1)} %convolution_bitcast_fusion.5), channel_id=1, replica_groups=mesh['sub'=8,'slab'=4] {'slab'}, use_global_device_ids=true, to_apply=%region_12.15 | all-reduce | flops 256 | bytes 2048 | tf_op jit(solution)/shard_map/psum | solution.py:131
  341.6 33.9 %all-reduce.87 = (f32[3,8,8]{2,1,0:T(8,128)S(1)}, f32[8,8]{0,1:T(8,128)S(1)}) all-reduce(f32[3,8,8]{2,1,0:T(8,128)S(1)} %get-tuple-element.196, f32[8,8]{0,1:T(8,128)S(1)} %get-tuple-element.197), channel_id=1, replica_groups=mesh['sub'=8,'slab'=4] {'sub'}, use_global_device_ids=true, to_apply=%region_13.16 | all-reduce | flops 256 | bytes 2048 | tf_op jit(solution)/shard_map/psum | solution.py:130
  420.7 4.2 collective-permute-done.60
  435.6 4.2 collective-permute-done.64
  443.8 10.3 %all-reduce.90 = (f32[4,8,8]{2,1,0:T(8,128)S(1)}, f32[8,8]{0,1:T(8,128)S(1)}) all-reduce(f32[4,8,8]{2,1,0:T(8,128)S(1)} %pad_maximum_fusion.42, f32[8,8]{0,1:T(8,128)S(1)} %convolution_bitcast_fusion), channel_id=1, replica_groups=mesh['sub'=8,'slab'=4] {'slab'}, use_global_device_ids=true, to_apply=%region_16.19 | all-reduce | flops 320 | bytes 2560 | tf_op jit(solution)/shard_map/psum | solution.py:131
  454.0 33.8 %all-reduce.86 = (f32[4,8,8]{2,1,0:T(8,128)S(1)}, f32[8,8]{0,1:T(8,128)S(1)}) all-reduce(f32[4,8,8]{2,1,0:T(8,128)S(1)} %get-tuple-element.194, f32[8,8]{0,1:T(8,128)S(1)} %get-tuple-element.195), channel_id=1, replica_groups=mesh['sub'=8,'slab'=4] {'sub'}, use_global_device_ids=true, to_apply=%region_17.20 | all-reduce | flops 320 | bytes 2560 | tf_op jit(solution)/shard_map/psum | solution.py:130
  526.6 4.2 collective-permute-done.72
  541.5 4.2 collective-permute-done.76
  (391 shorter events, 294.9 us)
Async XLA Ops:
  1.6 61.9 %collective-permute-start.3 = (f32[1,8,8,1]{3,2,1,0:T(8,128)S(1)}, f32[1,8,8,1]{3,2,1,0:T(8,128)S(1)}, u32[]{:S(2)}, u32[]{:S(2)}) collective-permute-start(f32[1,8,8,1]{3,2,1,0:T(8,128)S(1)} %get-tuple-element.401), channel_id=1, source_target_pairs={{0,1},{1,2},{2,3},{4,5},{5,6},{6,7},{8,9},{9,10},{10,11},{12,13},{... | collective-permute-start | bytes 776 | tf_op jit(solution)/shard_map/ppermute | solution.py:21
  3.5 60.0 %collective-permute-start.2 = (f32[1,8,8,1]{3,2,1,0:T(8,128)S(1)}, f32[1,8,8,1]{3,2,1,0:T(8,128)S(1)}, u32[]{:S(2)}, u32[]{:S(2)}) collective-permute-start(f32[1,8,8,1]{3,2,1,0:T(8,128)S(1)} %get-tuple-element.400), channel_id=1, source_target_pairs={{1,0},{2,1},{3,2},{5,4},{6,5},{7,6},{9,8},{10,9},{11,10},{13,12},{... | collective-permute-start | bytes 776 | tf_op jit(solution)/shard_map/ppermute | solution.py:23
  9.1 54.5 %collective-permute-start.1 = (f32[1,1,8,128]{3,2,1,0:T(8,128)S(1)}, f32[1,1,8,128]{3,2,1,0:T(8,128)S(1)}, u32[]{:S(2)}, u32[]{:S(2)}) collective-permute-start(f32[1,1,8,128]{3,2,1,0:T(8,128)S(1)} %fusion.154), channel_id=1, source_target_pairs={{0,4},{4,8},{8,12},{12,16},{16,20},{20,24},{24,28},{1,5},{5,9},{9,... | collective-permute-start | bytes 12296 | tf_op jit(solution)/shard_map/ppermute | solution.py:21
  12.6 51.0 %collective-permute-start = (f32[1,1,8,128]{3,2,1,0:T(8,128)S(1)}, f32[1,1,8,128]{3,2,1,0:T(8,128)S(1)}, u32[]{:S(2)}, u32[]{:S(2)}) collective-permute-start(f32[1,1,8,128]{3,2,1,0:T(8,128)S(1)} %slice.1210), channel_id=1, source_target_pairs={{4,0},{8,4},{12,8},{16,12},{20,16},{24,20},{28,24},{5,1},{9,5},{13... | collective-permute-start | bytes 12296 | tf_op jit(solution)/shard_map/ppermute | solution.py:23
  64.4 10.3 %collective-permute-start.7 = (f32[8,8,8,1]{3,0,2,1:T(8,128)S(1)}, f32[8,8,8,1]{3,0,2,1:T(8,128)S(1)}, u32[]{:S(2)}, u32[]{:S(2)}) collective-permute-start(f32[8,8,8,1]{3,0,2,1:T(8,128)S(1)} %get-tuple-element.387), channel_id=1, source_target_pairs={{0,1},{1,2},{2,3},{4,5},{5,6},{6,7},{8,9},{9,10},{10,11},{12,13},{... | collective-permute-start | bytes 6152 | tf_op jit(solution)/shard_map/ppermute | solution.py:21
  79.6 11.4 %collective-permute-start.11 = (f32[8,8,8,1]{3,0,2,1:T(8,128)S(1)}, f32[8,8,8,1]{3,0,2,1:T(8,128)S(1)}, u32[]{:S(2)}, u32[]{:S(2)}) collective-permute-start(f32[8,8,8,1]{3,0,2,1:T(8,128)S(1)} %get-tuple-element.379), channel_id=1, source_target_pairs={{0,1},{1,2},{2,3},{4,5},{5,6},{6,7},{8,9},{9,10},{10,11},{12,13},{... | collective-permute-start | bytes 6152 | tf_op jit(solution)/shard_map/ppermute | solution.py:21
  81.6 9.4 %collective-permute-start.10 = (f32[8,8,8,1]{3,0,2,1:T(8,128)S(1)}, f32[8,8,8,1]{3,0,2,1:T(8,128)S(1)}, u32[]{:S(2)}, u32[]{:S(2)}) collective-permute-start(f32[8,8,8,1]{3,0,2,1:T(8,128)S(1)} %get-tuple-element.378), channel_id=1, source_target_pairs={{1,0},{2,1},{3,2},{5,4},{6,5},{7,6},{9,8},{10,9},{11,10},{13,12},{... | collective-permute-start | bytes 6152 | tf_op jit(solution)/shard_map/ppermute | solution.py:23
  96.1 10.3 %collective-permute-start.15 = (f32[8,8,8,1]{3,0,2,1:T(8,128)S(1)}, f32[8,8,8,1]{3,0,2,1:T(8,128)S(1)}, u32[]{:S(2)}, u32[]{:S(2)}) collective-permute-start(f32[8,8,8,1]{3,0,2,1:T(8,128)S(1)} %get-tuple-element.371), channel_id=1, source_target_pairs={{0,1},{1,2},{2,3},{4,5},{5,6},{6,7},{8,9},{9,10},{10,11},{12,13},{... | collective-permute-start | bytes 6152 | tf_op jit(solution)/shard_map/ppermute | solution.py:21
  111.5 11.1 %collective-permute-start.19 = (f32[8,8,8,1]{3,0,2,1:T(8,128)S(1)}, f32[8,8,8,1]{3,0,2,1:T(8,128)S(1)}, u32[]{:S(2)}, u32[]{:S(2)}) collective-permute-start(f32[8,8,8,1]{3,0,2,1:T(8,128)S(1)} %get-tuple-element.363), channel_id=1, source_target_pairs={{0,1},{1,2},{2,3},{4,5},{5,6},{6,7},{8,9},{9,10},{10,11},{12,13},{... | collective-permute-start | bytes 6152 | tf_op jit(solution)/shard_map/ppermute | solution.py:21
  160.2 11.2 %collective-permute-start.23 = (f32[8,8,8,1]{3,0,2,1:T(8,128)}, f32[8,8,8,1]{3,0,2,1:T(8,128)S(1)}, u32[]{:S(2)}, u32[]{:S(2)}) collective-permute-start(f32[8,8,8,1]{3,0,2,1:T(8,128)} %get-tuple-element.355), channel_id=1, source_target_pairs={{0,1},{1,2},{2,3},{4,5},{5,6},{6,7},{8,9},{9,10},{10,11},{12,13},{... | collective-permute-start | bytes 6152 | tf_op jit(solution)/shard_map/ppermute | solution.py:21
  174.6 9.8 %collective-permute-start.27 = (f32[8,8,8,1]{3,0,2,1:T(8,128)S(1)}, f32[8,8,8,1]{3,0,2,1:T(8,128)S(1)}, u32[]{:S(2)}, u32[]{:S(2)}) collective-permute-start(f32[8,8,8,1]{3,0,2,1:T(8,128)S(1)} %get-tuple-element.347), channel_id=1, source_target_pairs={{0,1},{1,2},{2,3},{4,5},{5,6},{6,7},{8,9},{9,10},{10,11},{12,13},{... | collective-permute-start | bytes 6152 | tf_op jit(solution)/shard_map/ppermute | solution.py:21
  189.4 9.8 %collective-permute-start.31 = (f32[8,8,8,1]{3,0,2,1:T(8,128)S(1)}, f32[8,8,8,1]{3,0,2,1:T(8,128)S(1)}, u32[]{:S(2)}, u32[]{:S(2)}) collective-permute-start(f32[8,8,8,1]{3,0,2,1:T(8,128)S(1)} %get-tuple-element.339), channel_id=1, source_target_pairs={{0,1},{1,2},{2,3},{4,5},{5,6},{6,7},{8,9},{9,10},{10,11},{12,13},{... | collective-permute-start | bytes 6152 | tf_op jit(solution)/shard_map/ppermute | solution.py:21
  204.4 9.9 %collective-permute-start.35 = (f32[8,8,8,1]{3,0,2,1:T(8,128)S(1)}, f32[8,8,8,1]{3,0,2,1:T(8,128)S(1)}, u32[]{:S(2)}, u32[]{:S(2)}) collective-permute-start(f32[8,8,8,1]{3,0,2,1:T(8,128)S(1)} %get-tuple-element.331), channel_id=1, source_target_pairs={{0,1},{1,2},{2,3},{4,5},{5,6},{6,7},{8,9},{9,10},{10,11},{12,13},{... | collective-permute-start | bytes 6152 | tf_op jit(solution)/shard_map/ppermute | solution.py:21
  270.2 9.8 %collective-permute-start.39 = (f32[8,8,8,1]{3,0,2,1:T(8,128)}, f32[8,8,8,1]{3,0,2,1:T(8,128)S(1)}, u32[]{:S(2)}, u32[]{:S(2)}) collective-permute-start(f32[8,8,8,1]{3,0,2,1:T(8,128)} %get-tuple-element.323), channel_id=1, source_target_pairs={{0,1},{1,2},{2,3},{4,5},{5,6},{6,7},{8,9},{9,10},{10,11},{12,13},{... | collective-permute-start | bytes 6152 | tf_op jit(solution)/shard_map/ppermute | solution.py:21
  283.5 10.6 %collective-permute-start.43 = (f32[8,8,8,1]{3,0,2,1:T(8,128)S(1)}, f32[8,8,8,1]{3,0,2,1:T(8,128)S(1)}, u32[]{:S(2)}, u32[]{:S(2)}) collective-permute-start(f32[8,8,8,1]{3,0,2,1:T(8,128)S(1)} %get-tuple-element.315), channel_id=1, source_target_pairs={{0,1},{1,2},{2,3},{4,5},{5,6},{6,7},{8,9},{9,10},{10,11},{12,13},{... | collective-permute-start | bytes 6152 | tf_op jit(solution)/shard_map/ppermute | solution.py:21
  299.2 9.8 %collective-permute-start.47 = (f32[8,8,8,1]{3,0,2,1:T(8,128)S(1)}, f32[8,8,8,1]{3,0,2,1:T(8,128)S(1)}, u32[]{:S(2)}, u32[]{:S(2)}) collective-permute-start(f32[8,8,8,1]{3,0,2,1:T(8,128)S(1)} %get-tuple-element.307), channel_id=1, source_target_pairs={{0,1},{1,2},{2,3},{4,5},{5,6},{6,7},{8,9},{9,10},{10,11},{12,13},{... | collective-permute-start | bytes 6152 | tf_op jit(solution)/shard_map/ppermute | solution.py:21
  314.0 9.8 %collective-permute-start.51 = (f32[8,8,8,1]{3,0,2,1:T(8,128)S(1)}, f32[8,8,8,1]{3,0,2,1:T(8,128)S(1)}, u32[]{:S(2)}, u32[]{:S(2)}) collective-permute-start(f32[8,8,8,1]{3,0,2,1:T(8,128)S(1)} %get-tuple-element.299), channel_id=1, source_target_pairs={{0,1},{1,2},{2,3},{4,5},{5,6},{6,7},{8,9},{9,10},{10,11},{12,13},{... | collective-permute-start | bytes 6152 | tf_op jit(solution)/shard_map/ppermute | solution.py:21
  381.3 10.5 %collective-permute-start.55 = (f32[8,8,8,1]{3,0,2,1:T(8,128)}, f32[8,8,8,1]{3,0,2,1:T(8,128)S(1)}, u32[]{:S(2)}, u32[]{:S(2)}) collective-permute-start(f32[8,8,8,1]{3,0,2,1:T(8,128)} %get-tuple-element.291), channel_id=1, source_target_pairs={{0,1},{1,2},{2,3},{4,5},{5,6},{6,7},{8,9},{9,10},{10,11},{12,13},{... | collective-permute-start | bytes 6152 | tf_op jit(solution)/shard_map/ppermute | solution.py:21
  394.5 10.6 %collective-permute-start.59 = (f32[8,8,8,1]{3,0,2,1:T(8,128)S(1)}, f32[8,8,8,1]{3,0,2,1:T(8,128)S(1)}, u32[]{:S(2)}, u32[]{:S(2)}) collective-permute-start(f32[8,8,8,1]{3,0,2,1:T(8,128)S(1)} %get-tuple-element.283), channel_id=1, source_target_pairs={{0,1},{1,2},{2,3},{4,5},{5,6},{6,7},{8,9},{9,10},{10,11},{12,13},{... | collective-permute-start | bytes 6152 | tf_op jit(solution)/shard_map/ppermute | solution.py:21
  410.2 10.3 %collective-permute-start.63 = (f32[8,8,8,1]{3,0,2,1:T(8,128)S(1)}, f32[8,8,8,1]{3,0,2,1:T(8,128)S(1)}, u32[]{:S(2)}, u32[]{:S(2)}) collective-permute-start(f32[8,8,8,1]{3,0,2,1:T(8,128)S(1)} %get-tuple-element.275), channel_id=1, source_target_pairs={{0,1},{1,2},{2,3},{4,5},{5,6},{6,7},{8,9},{9,10},{10,11},{12,13},{... | collective-permute-start | bytes 6152 | tf_op jit(solution)/shard_map/ppermute | solution.py:21
  425.6 9.8 %collective-permute-start.67 = (f32[8,8,8,1]{3,0,2,1:T(8,128)S(1)}, f32[8,8,8,1]{3,0,2,1:T(8,128)S(1)}, u32[]{:S(2)}, u32[]{:S(2)}) collective-permute-start(f32[8,8,8,1]{3,0,2,1:T(8,128)S(1)} %get-tuple-element.267), channel_id=1, source_target_pairs={{0,1},{1,2},{2,3},{4,5},{5,6},{6,7},{8,9},{9,10},{10,11},{12,13},{... | collective-permute-start | bytes 6152 | tf_op jit(solution)/shard_map/ppermute | solution.py:21
  515.9 10.5 %collective-permute-start.75 = (f32[8,8,8,1]{3,0,2,1:T(8,128)S(1)}, f32[8,8,8,1]{3,0,2,1:T(8,128)S(1)}, u32[]{:S(2)}, u32[]{:S(2)}) collective-permute-start(f32[8,8,8,1]{3,0,2,1:T(8,128)S(1)} %get-tuple-element.251), channel_id=1, source_target_pairs={{0,1},{1,2},{2,3},{4,5},{5,6},{6,7},{8,9},{9,10},{10,11},{12,13},{... | collective-permute-start | bytes 6152 | tf_op jit(solution)/shard_map/ppermute | solution.py:21
  531.5 9.8 %collective-permute-start.79 = (f32[8,8,8,1]{3,0,2,1:T(8,128)S(1)}, f32[8,8,8,1]{3,0,2,1:T(8,128)S(1)}, u32[]{:S(2)}, u32[]{:S(2)}) collective-permute-start(f32[8,8,8,1]{3,0,2,1:T(8,128)S(1)} %get-tuple-element.243), channel_id=1, source_target_pairs={{0,1},{1,2},{2,3},{4,5},{5,6},{6,7},{8,9},{9,10},{10,11},{12,13},{... | collective-permute-start | bytes 6152 | tf_op jit(solution)/shard_map/ppermute | solution.py:21
  546.4 10.5 %collective-permute-start.83 = (f32[8,8,8,1]{3,0,2,1:T(8,128)S(1)}, f32[8,8,8,1]{3,0,2,1:T(8,128)S(1)}, u32[]{:S(2)}, u32[]{:S(2)}) collective-permute-start(f32[8,8,8,1]{3,0,2,1:T(8,128)S(1)} %get-tuple-element.235), channel_id=1, source_target_pairs={{0,1},{1,2},{2,3},{4,5},{5,6},{6,7},{8,9},{9,10},{10,11},{12,13},{... | collective-permute-start | bytes 6152 | tf_op jit(solution)/shard_map/ppermute | solution.py:21
  (65 other events, 409.2 us)
